TPU v7x, 32 devices: a whole 2x2x4 slice. The times are simulated.
32 devices in a mesh: seq: 8 (over z, x), tp: 4 (over y, core).
Axes of the slice: x: 2, y: 2, z: 4, core: 2. Of those that a mesh axis runs over, the one named last changes fastest.
Arguments:
- tree_hidden: bfloat16 [16, 8192], P(None, 'seq'), may hold values from -6 to 6
- query_low: bfloat16 [16, 8192], P('seq', 'tp'), may hold values from -24 to 24
- key_tree_low: bfloat16 [16, 1024], P('seq', 'tp'), may hold values from -20 to 20
- value_tree_low: bfloat16 [16, 1024], P('seq', 'tp'), may hold values from -6 to 6
- cache_keys: bfloat16 [1, 8192, 8, 128], P(None, 'seq', 'tp'), may hold values from -40 to 40
- cache_values: bfloat16 [1, 8192, 8, 128], P(None, 'seq', 'tp'), may hold values from -6 to 6
- cache_lengths: int32 [1], replicated, may hold values from 1024 to 8192
- ancestors: int32 [1, 16, 16], replicated, may hold values from 0 to 1, as said below
- out_weight: bfloat16 [8192, 8192], P('tp', 'seq'), may hold values from -0.0625 to 0.0625
- norm_gain: float32 [8192], P('seq'), may hold values from 0.1 to 1.9
- w_query_up: bfloat16 [8192, 8192], P('seq', 'tp'), may hold values from -0.0625 to 0.0625
- w_key_up: bfloat16 [8192, 1024], P('seq', 'tp'), may hold values from -0.5 to 0.5
- w_value_up: bfloat16 [8192, 1024], P('seq', 'tp'), may hold values from -0.0625 to 0.0625
- retained_keys: bfloat16 [8, 512, 8, 128], P('seq', None, 'tp'), may hold values from -400 to 400
- retained_values: bfloat16 [8, 512, 8, 128], P('seq', None, 'tp'), may hold values from -6 to 6
- retained_index: int32 [8, 512, 8], P('seq', None, 'tp'), may hold values from 0 to 8191
Outputs:
- residual: float32 [16, 8192], P(None, 'seq')
- upper_heads: float32 [16, 8192], P('seq', 'tp')
Inputs may be any that keep to these rules, and one draw needn't show every extreme that they name: ancestors[r, i, j] is 1 when node j is node i or an ancestor of node i in request r's tree, else 0; node 0 is the root and every other node's parent has a lower number.
All inputs are finite; a program needn't handle non-finite values.
Results may differ from a plain program's by a relative error of at most 0.04.
Values may be sent and summed in bfloat16 or wider, within the bound.
A program may use at most 64 MiB of HBM per device.

v0:
```python
import jax
import jax.numpy as jnp
from jax import lax
from jax.sharding import PartitionSpec as P

GROUP = 8


masked_score = -1e30
norm_epsilon = 1e-05


def swapped(array, axis, apart):
    return lax.ppermute(array, axis, [(i, i ^ 1 << apart) for i in range(lax.axis_size(axis))])


def block_attend(query_rows, key_rows, value_rows, allowed_keys, kv_heads, head_dim):
    row_count = query_rows.shape[0]
    head_count = query_rows.shape[1] // head_dim
    group_size = head_count // kv_heads
    queries = query_rows.reshape(row_count, kv_heads, group_size, head_dim)
    scores = jnp.einsum(
        "nkgd,ckd->kgnc", queries, key_rows, preferred_element_type=jnp.float32
    ) * head_dim ** (-0.5)
    allowed = allowed_keys.T[:, None, None, :]
    masked = jnp.where(allowed, scores, masked_score)
    highest = jnp.max(masked, axis=-1)
    weights = jnp.where(allowed, jnp.exp(masked - highest[..., None]), 0.0)
    weight_sum = jnp.sum(weights, axis=-1)
    blended = jnp.einsum(
        "kgnc,ckd->nkgd",
        weights.astype(jnp.bfloat16),
        value_rows,
        preferred_element_type=jnp.float32,
    )
    return (
        blended.reshape(row_count, head_count, head_dim),
        highest.transpose(2, 0, 1).reshape(row_count, head_count),
        weight_sum.transpose(2, 0, 1).reshape(row_count, head_count),
    )


def tree_attend(query_rows, key_rows, value_rows, mask_rows, kv_heads, head_dim):
    row_count = query_rows.shape[0]
    head_count = query_rows.shape[1] // head_dim
    group_size = head_count // kv_heads
    queries = query_rows.reshape(row_count, kv_heads, group_size, head_dim)
    tree_keys = key_rows.reshape(-1, kv_heads, head_dim)
    tree_values = value_rows.reshape(-1, kv_heads, head_dim)
    scores = jnp.einsum(
        "nkgd,mkd->nkgm", queries, tree_keys, preferred_element_type=jnp.float32
    ) * head_dim ** (-0.5)
    allowed = (mask_rows > 0)[:, None, None, :]
    masked = jnp.where(allowed, scores, masked_score)
    highest = jnp.max(masked, axis=-1)
    weights = jnp.where(allowed, jnp.exp(masked - highest[..., None]), 0.0)
    weight_sum = jnp.sum(weights, axis=-1)
    blended = jnp.einsum(
        "nkgm,mkd->nkgd",
        weights.astype(jnp.bfloat16),
        tree_values,
        preferred_element_type=jnp.float32,
    )
    return (
        blended.reshape(row_count, head_count, head_dim),
        highest.reshape(row_count, head_count),
        weight_sum.reshape(row_count, head_count),
    )


def combine_parts(earlier, later):
    blend_early, high_early, sum_early = earlier
    blend_late, high_late, sum_late = later
    highest = jnp.maximum(high_early, high_late)
    factor_early = jnp.exp(high_early - highest)
    factor_late = jnp.exp(high_late - highest)
    return (
        blend_early * factor_early[..., None] + blend_late * factor_late[..., None],
        highest,
        sum_early * factor_early + sum_late * factor_late,
    )


def finish(partial_value, out_type):
    blended, highest, weight_sum = partial_value
    return (blended / weight_sum[..., None]).reshape(blended.shape[0], -1).astype(out_type)


def ordered_pair(mine, partner, upper_half):
    return jnp.where(
        upper_half,
        jnp.concatenate([partner, mine], axis=0),
        jnp.concatenate([mine, partner], axis=0),
    )


def shards(
    tree_hidden,
    query_low,
    key_tree_low,
    value_tree_low,
    cache_keys,
    cache_values,
    cache_lengths,
    ancestors,
    out_weight,
    norm_gain,
    w_query_up,
    w_key_up,
    w_value_up,
    retained_keys,
    retained_values,
    retained_index,
):
    seq_count = lax.axis_size("seq")
    seq_index = lax.axis_index("seq")
    requests, cache_part, kv_heads, head_dim = cache_keys.shape
    node_count = ancestors.shape[1]
    own_rows = query_low.shape[0]
    row_width = query_low.shape[1]
    all_rows = requests * node_count
    first_row = seq_index * own_rows
    request = first_row // node_count
    node_start = first_row % node_count
    tree_mask = lax.dynamic_slice_in_dim(
        lax.dynamic_index_in_dim(ancestors, request, 0, keepdims=False), node_start, own_rows, 0
    )
    seq_length = jnp.sum(
        jnp.where(jnp.arange(requests, dtype=jnp.int32) == request, cache_lengths, 0)
    )
    gathered_q, gathered_k, gathered_v = (
        lax.all_gather(query_low, "seq", axis=0, tiled=True),
        lax.all_gather(key_tree_low, "seq", axis=0, tiled=True),
        lax.all_gather(value_tree_low, "seq", axis=0, tiled=True),
    )
    positions = seq_index * cache_part + jnp.arange(cache_part, dtype=jnp.int32)

    def cache_request(operands):
        query_rows, key_rows, value_rows, length_here = operands
        usable = jnp.broadcast_to((positions < length_here)[:, None], (cache_part, kv_heads))
        return block_attend(query_rows, key_rows, value_rows, usable, kv_heads, head_dim)

    part_blend, part_high, part_sum = lax.map(
        cache_request,
        (
            gathered_q.reshape(requests, node_count, row_width),
            cache_keys,
            cache_values,
            cache_lengths,
        ),
    )
    part_blend = part_blend.reshape(all_rows, -1, head_dim)
    part_high = part_high.reshape(all_rows, -1)
    part_sum = part_sum.reshape(all_rows, -1)
    spread_blend, spread_high, spread_sum = (
        lax.all_to_all(part_blend[None], "seq", split_axis=1, concat_axis=0, tiled=True),
        lax.all_to_all(part_high[None], "seq", split_axis=1, concat_axis=0, tiled=True),
        lax.all_to_all(part_sum[None], "seq", split_axis=1, concat_axis=0, tiled=True),
    )
    highest = jnp.max(spread_high, axis=0)
    factor = jnp.exp(spread_high - highest[None])
    cache_merged = (
        jnp.sum(spread_blend * factor[..., None], axis=0),
        highest,
        jnp.sum(spread_sum * factor, axis=0),
    )
    request_keys = lax.dynamic_slice_in_dim(gathered_k, request * node_count, node_count, 0)
    request_values = lax.dynamic_slice_in_dim(gathered_v, request * node_count, node_count, 0)
    own_heads = finish(
        combine_parts(
            cache_merged,
            tree_attend(query_low, request_keys, request_values, tree_mask, kv_heads, head_dim),
        ),
        jnp.bfloat16,
    )
    lower_all = lax.all_gather(own_heads, "seq", axis=0, tiled=True)
    head_terms = jnp.dot(lower_all, out_weight, preferred_element_type=jnp.float32)
    summed = lax.psum(head_terms, "tp")
    residual = tree_hidden.astype(jnp.float32) + summed
    squares = lax.psum(jnp.sum(residual * residual, axis=1), "seq")
    model_width = residual.shape[1] * seq_count
    inverse = lax.rsqrt(squares / model_width + norm_epsilon)
    normed = (residual * inverse[:, None] * norm_gain[None, :]).astype(jnp.bfloat16)
    projected = lax.psum_scatter(
        jnp.concatenate(
            [
                jnp.dot(normed, w_query_up, preferred_element_type=jnp.float32),
                jnp.dot(normed, w_key_up, preferred_element_type=jnp.float32),
                jnp.dot(normed, w_value_up, preferred_element_type=jnp.float32),
            ],
            axis=1,
        ),
        "seq",
        scatter_dimension=0,
        tiled=True,
    )
    kv_width = w_key_up.shape[1]
    query_up = projected[:, :row_width].astype(jnp.bfloat16)
    key_up = projected[:, row_width : row_width + kv_width].astype(jnp.bfloat16)
    value_up = projected[:, row_width + kv_width :].astype(jnp.bfloat16)
    levels = GROUP.bit_length() - 1
    keys_here = retained_keys[0]
    values_here = retained_values[0]
    index_here = retained_index[0]
    rows_query, rows_key, rows_value = (query_up, key_up, value_up)
    for level in range(levels):
        other_query, other_key, other_value = swapped(
            (rows_query, rows_key, rows_value), "seq", level
        )
        upper_half = jnp.right_shift(seq_index, level) % 2 == 1
        rows_query = ordered_pair(rows_query, other_query, upper_half)
        rows_key = ordered_pair(rows_key, other_key, upper_half)
        rows_value = ordered_pair(rows_value, other_value, upper_half)
    partial_value = block_attend(
        rows_query, keys_here, values_here, index_here < seq_length, kv_heads, head_dim
    )
    for level in range(levels):
        partner = swapped((partial_value[0], partial_value[1], partial_value[2]), "seq", level)
        partial_value = combine_parts(partial_value, partner)
    own_parts = (
        lax.dynamic_slice_in_dim(partial_value[0], node_start, own_rows, 0),
        lax.dynamic_slice_in_dim(partial_value[1], node_start, own_rows, 0),
        lax.dynamic_slice_in_dim(partial_value[2], node_start, own_rows, 0),
    )
    upper_heads = finish(
        combine_parts(
            own_parts, tree_attend(query_up, rows_key, rows_value, tree_mask, kv_heads, head_dim)
        ),
        jnp.float32,
    )
    return (residual, upper_heads)


def solution(mesh):
    return jax.shard_map(
        shards,
        mesh=mesh,
        in_specs=(
            P(None, "seq"),
            P("seq", "tp"),
            P("seq", "tp"),
            P("seq", "tp"),
            P(None, "seq", "tp", None),
            P(None, "seq", "tp", None),
            P(),
            P(),
            P("tp", "seq"),
            P("seq"),
            P("seq", "tp"),
            P("seq", "tp"),
            P("seq", "tp"),
            P("seq", None, "tp", None),
            P("seq", None, "tp", None),
            P("seq", None, "tp"),
        ),
        out_specs=(P(None, "seq"), P("seq", "tp")),
        check_vma=False,
    )
```

profile of v0, /device:TPU:0, one launch (start us, length us, event | category | flops | bytes accessed | tf_op | source)
XLA Modules:
  0.0 292.4 jit_solution(13074461663590758991)
XLA Ops:
  7.9 32.6 %all-gather = bf16[8,2,2048]{2,1,0:T(2,128)(2,1)S(1)} all-gather(bf16[1,2,2048]{2,1,0:T(2,128)(2,1)} %bitcast.203), channel_id=1, replica_groups=mesh['seq'=8,'tp'=4] {'seq'}, dimensions={0}, use_global_device_ids=true | all-gather | bytes 73728 | tf_op jit(solution)/shard_map/all_gather | solution.py:132
  40.5 0.4 fusion.85
  41.0 0.7 copy.324
  41.7 5.5 %all-to-all-start.1 = ((f32[1,16,16]{2,0,1:T(1,128)}), f32[1,16,16]{2,0,1:T(1,128)S(1)}, u32[]{:S(2)}, u32[]{:S(2)}) async-start(f32[1,16,16]{2,0,1:T(1,128)} %copy.324), calls=%async_computation.1 | async-start | bytes 16384 | tf_op jit(solution)/shard_map/all_to_all | solution.py:157
  47.1 21.2 %all-gather.1 = bf16[8,2,256]{2,1,0:T(2,128)(2,1)S(1)} all-gather(bf16[1,2,256]{2,1,0:T(2,128)(2,1)} %bitcast.211), channel_id=1, replica_groups=mesh['seq'=8,'tp'=4] {'seq'}, dimensions={0}, use_global_device_ids=true | all-gather | bytes 9216 | tf_op jit(solution)/shard_map/all_gather | solution.py:133
  68.4 16.6 %all-gather.2 = bf16[8,2,256]{2,1,0:T(2,128)(2,1)S(1)} all-gather(bf16[1,2,256]{2,1,0:T(2,128)(2,1)} %bitcast.212), channel_id=1, replica_groups=mesh['seq'=8,'tp'=4] {'seq'}, dimensions={0}, use_global_device_ids=true | all-gather | bytes 9216 | tf_op jit(solution)/shard_map/all_gather | solution.py:134
  85.0 0.7 compare_bitcast_fusion.1
  85.7 1.4 convolution_bitcast_fusion
  87.2 0.9 fusion.84
  88.1 0.2 convolution_bitcast_fusion.2
  88.3 0.3 fusion.8
  88.7 0.7 copy.331
  89.4 3.3 %all-to-all-start.2 = ((f32[1,16,16]{2,0,1:T(1,128)}), f32[1,16,16]{2,0,1:T(1,128)S(1)}, u32[]{:S(2)}, u32[]{:S(2)}) async-start(f32[1,16,16]{2,0,1:T(1,128)} %copy.331), calls=%async_computation.2 | async-start | bytes 16384 | tf_op jit(solution)/shard_map/all_to_all | solution.py:158
  92.7 0.2 fusion.31
  93.0 0.7 copy.462
  93.7 5.4 %all-to-all-done.2 = f32[1,16,16]{2,0,1:T(1,128)S(1)} async-done(((f32[1,16,16]{2,0,1:T(1,128)}), f32[1,16,16]{2,0,1:T(1,128)S(1)}, u32[]{:S(2)}, u32[]{:S(2)}) %all-to-all-start.2) | async-done | bytes 1056 | tf_op jit(solution)/shard_map/all_to_all | solution.py:158
  99.2 3.4 %all-to-all-start = ((f32[1,16,16,128]{3,2,0,1:T(8,128)}), f32[1,16,16,128]{3,2,0,1:T(8,128)S(1)}, u32[]{:S(2)}, u32[]{:S(2)}) async-start(f32[1,16,16,128]{3,2,0,1:T(8,128)} %bitcast.171), calls=%async_computation | async-start | bytes 262144 | tf_op jit(solution)/shard_map/all_to_all | solution.py:156
  102.7 7.1 %all-to-all-done = f32[1,16,16,128]{3,2,0,1:T(8,128)S(1)} async-done(((f32[1,16,16,128]{3,2,0,1:T(8,128)}), f32[1,16,16,128]{3,2,0,1:T(8,128)S(1)}, u32[]{:S(2)}, u32[]{:S(2)}) %all-to-all-start) | async-done | bytes 131104 | tf_op jit(solution)/shard_map/all_to_all | solution.py:156
  110.0 30.6 %all-gather.3 = bf16[8,2,2048]{2,1,0:T(2,128)(2,1)S(1)} all-gather(bf16[1,2,2048]{2,1,0:T(2,128)(2,1)S(1)} %fusion.63), channel_id=1, replica_groups=mesh['seq'=8,'tp'=4] {'seq'}, dimensions={0}, use_global_device_ids=true | all-gather | bytes 73728 | tf_op jit(solution)/shard_map/all_gather | solution.py:176
  140.7 3.6 %fusion.88 = f32[16,1024]{1,0:T(8,128)} fusion(bf16[16,2048]{1,0:T(8,128)(2,1)S(1)} %reshape.219, bf16[2048,1024]{1,0:T(8,128)(2,1)} %param.24), kind=kOutput, calls=%fused_computation.157 | convolution fusion | flops 67108864 | bytes 4325376 | tf_op jit(solution)/shard_map/dot_general | solution.py:177
  144.3 0.6 dynamic-slice.2
  145.5 28.2 %all-reduce.4.cloned.1.call-done = f32[16,1024]{1,0:T(8,128)} async-done(((f32[16,1024]{1,0:T(8,128)}), f32[16,1024]{1,0:T(8,128)}) %all-reduce.4.cloned.1.call-update) | async-done | bytes 65552 | tf_op jit(solution)/shard_map/psum | solution.py:178
  173.7 1.0 multiply_reduce_fusion.1
  174.7 21.4 %psum.15 = f32[16]{0:T(128)S(1)} all-reduce(f32[16]{0:T(128)S(1)} %get-tuple-element.44), channel_id=1, replica_groups=mesh['seq'=8,'tp'=4] {'seq'}, use_global_device_ids=true, to_apply=%region_9.10 | all-reduce | flops 16 | bytes 128 | tf_op jit(solution)/shard_map/psum | solution.py:180
  196.1 2.9 fusion.89
  199.0 0.2 fusion.90
  199.2 0.2 fusion.91
  199.4 34.8 %all-reduce.5 = bf16[16,2560]{1,0:T(8,128)(2,1)S(1)} all-reduce(f32[16,2560]{1,0:T(8,128)S(1)} %pad_maximum_fusion), channel_id=2, replica_groups=mesh['seq'=8,'tp'=4] {'seq'}, use_global_device_ids=true, to_apply=%region_10.11.clone | all-reduce | flops 40960 | bytes 245760
  234.3 2.1 collective-permute-start
  236.5 1.4 collective-permute-done.9
  238.0 2.0 collective-permute-done.12
  240.1 1.4 collective-permute-done.10
  241.6 2.0 collective-permute-done.13
  243.7 1.0 collective-permute-start.14
  244.6 1.5 collective-permute-done.11
  246.1 0.2 fusion.87
  246.4 0.7 collective-permute-start.1
  247.1 3.1 %collective-permute-done.1 = bf16[4,2048]{1,0:T(4,128)(2,1)S(1)} collective-permute-done((bf16[4,2048]{1,0:T(4,128)(2,1)S(1)}, bf16[4,2048]{1,0:T(4,128)(2,1)S(1)}, u32[]{:S(2)}, u32[]{:S(2)}) %collective-permute-start.1) | collective-permute-done | bytes 16416 | tf_op jit(solution)/shard_map/ppermute | solution.py:14
  250.2 0.6 collective-permute-start.2
  250.9 4.5 %collective-permute-done.2 = bf16[8,2048]{1,0:T(8,128)(2,1)S(1)} collective-permute-done((bf16[8,2048]{1,0:T(8,128)(2,1)S(1)}, bf16[8,2048]{1,0:T(8,128)(2,1)S(1)}, u32[]{:S(2)}, u32[]{:S(2)}) %collective-permute-start.2) | collective-permute-done | bytes 32800 | tf_op jit(solution)/shard_map/ppermute | solution.py:14
  255.4 0.3 fusion.86
  255.8 0.2 fusion.16
  256.1 0.2 collective-permute-start.15
  256.5 1.8 collective-permute-start.3
  258.3 0.2 convolution_bitcast_fusion.1
  258.5 1.3 collective-permute-done.15
  259.8 0.4 collective-permute-done.3
  260.2 0.5 collective-permute-start.16
  260.7 1.6 collective-permute-start.5
  262.3 0.2 fusion.33
  262.6 1.3 collective-permute-done.16
  263.9 0.4 collective-permute-done.5
  264.3 2.5 collective-permute-start.7
  266.8 0.2 fusion.18
  267.1 0.4 collective-permute-start.4
  267.6 2.1 collective-permute-start.17
  269.7 2.5 collective-permute-done.4
  272.2 0.1 multiply_add_fusion.1
  272.3 0.7 collective-permute-start.6
  273.0 4.3 %collective-permute-done.6 = f32[16,16,128]{2,1,0:T(8,128)S(1)} collective-permute-done((f32[16,16,128]{2,1,0:T(8,128)S(1)}, f32[16,16,128]{2,1,0:T(8,128)S(1)}, u32[]{:S(2)}, u32[]{:S(2)}) %collective-permute-start.6) | collective-permute-done | bytes 131104 | tf_op jit(solution)/shard_map/ppermute | solution.py:14
  277.3 0.1 multiply_add_fusion
  277.5 0.5 collective-permute-start.8
  278.0 6.8 %collective-permute-done.8 = f32[16,16,128]{2,1,0:T(8,128)S(1)} collective-permute-done((f32[16,16,128]{2,1,0:T(8,128)S(1)}, f32[16,16,128]{2,1,0:T(8,128)S(1)}, u32[]{:S(2)}, u32[]{:S(2)}) %collective-permute-start.8) | collective-permute-done | bytes 131104 | tf_op jit(solution)/shard_map/ppermute | solution.py:14
  284.9 0.6 copy.464
  (89 shorter events, 2.2 us)
Async XLA Ops:
  7.2 33.4 %copy-start = (bf16[1,1024,2,128]{3,2,1,0:T(2,128)(2,1)S(1)}, bf16[1,1024,2,128]{3,2,1,0:T(2,128)(2,1)}, u32[]{:S(2)}) copy-start(bf16[1,1024,2,128]{3,2,1,0:T(2,128)(2,1)} %param.20) | copy-start | bytes 1572868
  41.7 47.7 %all-to-all-start.1 = ((f32[1,16,16]{2,0,1:T(1,128)}), f32[1,16,16]{2,0,1:T(1,128)S(1)}, u32[]{:S(2)}, u32[]{:S(2)}) async-start(f32[1,16,16]{2,0,1:T(1,128)} %copy.324), calls=%async_computation.1 | async-start | bytes 16384 | tf_op jit(solution)/shard_map/all_to_all | solution.py:157
  85.7 58.5 %copy-start.6 = (s32[1,512,2]{1,2,0:T(2,128)S(1)}, s32[1,512,2]{1,2,0:T(2,128)}, u32[]{:S(2)}) copy-start(s32[1,512,2]{1,2,0:T(2,128)} %param.31) | copy-start | bytes 12292
  85.7 58.6 %copy-start.9 = (u32[32]{0:T(128)S(1)}, u32[32]{0:T(128)}, u32[]{:S(2)}) copy-start(u32[32]{0:T(128)} %constant.111) | copy-start | bytes 388
  85.7 88.0 %copy-start.4 = (bf16[16,1024]{1,0:T(8,128)(2,1)S(1)}, bf16[16,1024]{1,0:T(8,128)(2,1)}, u32[]{:S(2)}) copy-start(bf16[16,1024]{1,0:T(8,128)(2,1)} %param.16) | copy-start | bytes 98308
  85.7 110.3 %copy-start.5 = (f32[1024]{0:T(1024)S(1)}, f32[1024]{0:T(1024)}, u32[]{:S(2)}) copy-start(f32[1024]{0:T(1024)} %param.25) | copy-start | bytes 12292
  89.4 9.8 %all-to-all-start.2 = ((f32[1,16,16]{2,0,1:T(1,128)}), f32[1,16,16]{2,0,1:T(1,128)S(1)}, u32[]{:S(2)}, u32[]{:S(2)}) async-start(f32[1,16,16]{2,0,1:T(1,128)} %copy.331), calls=%async_computation.2 | async-start | bytes 16384 | tf_op jit(solution)/shard_map/all_to_all | solution.py:158
  99.2 10.7 %all-to-all-start = ((f32[1,16,16,128]{3,2,0,1:T(8,128)}), f32[1,16,16,128]{3,2,0,1:T(8,128)S(1)}, u32[]{:S(2)}, u32[]{:S(2)}) async-start(f32[1,16,16,128]{3,2,0,1:T(8,128)} %bitcast.171), calls=%async_computation | async-start | bytes 262144 | tf_op jit(solution)/shard_map/all_to_all | solution.py:156
  102.5 71.2 %all-reduce.4.cloned.1.call-start = ((), (), s32[]{:S(2)}) async-start(), calls=%async_computation.3 | async-start | bytes 131072 | tf_op jit(solution)/shard_map/psum | solution.py:178
  140.6 58.4 %copy-start.1 = (bf16[1024,256]{1,0:T(8,128)(2,1)S(1)}, bf16[1024,256]{1,0:T(8,128)(2,1)}, u32[]{:S(2)}) copy-start(bf16[1024,256]{1,0:T(8,128)(2,1)} %param.27) | copy-start | bytes 1572868
  140.6 58.6 %copy-start.2 = (bf16[1024,256]{1,0:T(8,128)(2,1)S(1)}, bf16[1024,256]{1,0:T(8,128)(2,1)}, u32[]{:S(2)}) copy-start(bf16[1024,256]{1,0:T(8,128)(2,1)} %param.28) | copy-start | bytes 1572868
  144.2 111.2 %copy-start.7 = (bf16[1,512,2,128]{3,2,1,0:T(2,128)(2,1)S(1)}, bf16[1,512,2,128]{3,2,1,0:T(2,128)(2,1)}, u32[]{:S(2)}) copy-start(bf16[1,512,2,128]{3,2,1,0:T(2,128)(2,1)} %param.29) | copy-start | bytes 786436
  174.7 81.3 %copy-start.3 = (f32[16,1024]{1,0:T(8,128)}, f32[16,1024]{1,0:T(8,128)S(1)}, u32[]{:S(2)}) copy-start(f32[16,1024]{1,0:T(8,128)S(1)} %get-tuple-element.45) | copy-start | bytes 196612
  196.1 70.7 %copy-start.8 = (bf16[1,512,2,128]{3,2,1,0:T(2,128)(2,1)S(1)}, bf16[1,512,2,128]{3,2,1,0:T(2,128)(2,1)}, u32[]{:S(2)}) copy-start(bf16[1,512,2,128]{3,2,1,0:T(2,128)(2,1)} %param.30) | copy-start | bytes 786436
  234.2 3.6 %collective-permute-start.9 = (bf16[2,256]{1,0:T(2,128)(2,1)S(1)}, bf16[2,256]{1,0:T(2,128)(2,1)S(1)}, u32[]{:S(2)}, u32[]{:S(2)}) collective-permute-start(bf16[2,256]{1,0:T(2,128)(2,1)S(1)} %get-tuple-element.56), channel_id=1, source_target_pairs={{0,4},{4,0},{8,12},{12,8},{16,20},{20,16},{24,28},{28,24},{1,5},{5... | collective-permute-start | bytes 3080 | tf_op jit(solution)/shard_map/ppermute | solution.py:14
  234.3 12.0 %collective-permute-start = (bf16[2,2048]{1,0:T(2,128)(2,1)S(1)}, bf16[2,2048]{1,0:T(2,128)(2,1)S(1)}, u32[]{:S(2)}, u32[]{:S(2)}) collective-permute-start(bf16[2,2048]{1,0:T(2,128)(2,1)S(1)} %get-tuple-element.57), channel_id=1, source_target_pairs={{0,4},{4,0},{8,12},{12,8},{16,20},{20,16},{24,28},{28,24},{1,5},{5... | collective-permute-start | bytes 24584 | tf_op jit(solution)/shard_map/ppermute | solution.py:14
  236.4 3.6 %collective-permute-start.12 = (bf16[2,256]{1,0:T(2,128)(2,1)S(1)}, bf16[2,256]{1,0:T(2,128)(2,1)S(1)}, u32[]{:S(2)}, u32[]{:S(2)}) collective-permute-start(bf16[2,256]{1,0:T(2,128)(2,1)S(1)} %get-tuple-element.53), channel_id=1, source_target_pairs={{0,4},{4,0},{8,12},{12,8},{16,20},{20,16},{24,28},{28,24},{1,5},{5... | collective-permute-start | bytes 3080 | tf_op jit(solution)/shard_map/ppermute | solution.py:14
  237.9 3.7 %collective-permute-start.10 = (bf16[4,256]{1,0:T(4,128)(2,1)S(1)}, bf16[4,256]{1,0:T(4,128)(2,1)S(1)}, u32[]{:S(2)}, u32[]{:S(2)}) collective-permute-start(bf16[4,256]{1,0:T(4,128)(2,1)S(1)} %maximum_select_fusion.11), channel_id=1, source_target_pairs={{0,8},{4,12},{8,0},{12,4},{16,24},{20,28},{24,16},{28,20},{1,9},{5... | collective-permute-start | bytes 6152 | tf_op jit(solution)/shard_map/ppermute | solution.py:14
  240.0 3.7 %collective-permute-start.13 = (bf16[4,256]{1,0:T(4,128)(2,1)S(1)}, bf16[4,256]{1,0:T(4,128)(2,1)S(1)}, u32[]{:S(2)}, u32[]{:S(2)}) collective-permute-start(bf16[4,256]{1,0:T(4,128)(2,1)S(1)} %maximum_select_fusion.13), channel_id=1, source_target_pairs={{0,8},{4,12},{8,0},{12,4},{16,24},{20,28},{24,16},{28,20},{1,9},{5... | collective-permute-start | bytes 6152 | tf_op jit(solution)/shard_map/ppermute | solution.py:14
  241.5 4.6 %collective-permute-start.11 = (bf16[8,256]{1,0:T(8,128)(2,1)S(1)}, bf16[8,256]{1,0:T(8,128)(2,1)S(1)}, u32[]{:S(2)}, u32[]{:S(2)}) collective-permute-start(bf16[8,256]{1,0:T(8,128)(2,1)S(1)} %maximum_select_fusion.7), channel_id=1, source_target_pairs={{0,16},{4,20},{8,24},{12,28},{16,0},{20,4},{24,8},{28,12},{1,17},{... | collective-permute-start | bytes 12296 | tf_op jit(solution)/shard_map/ppermute | solution.py:14
  243.7 14.7 %collective-permute-start.14 = (bf16[8,256]{1,0:T(8,128)(2,1)S(1)}, bf16[8,256]{1,0:T(8,128)(2,1)S(1)}, u32[]{:S(2)}, u32[]{:S(2)}) collective-permute-start(bf16[8,256]{1,0:T(8,128)(2,1)S(1)} %maximum_select_fusion.9), channel_id=1, source_target_pairs={{0,16},{4,20},{8,24},{12,28},{16,0},{20,4},{24,8},{28,12},{1,17},{... | collective-permute-start | bytes 12296 | tf_op jit(solution)/shard_map/ppermute | solution.py:14
  246.4 3.8 %collective-permute-start.1 = (bf16[4,2048]{1,0:T(4,128)(2,1)S(1)}, bf16[4,2048]{1,0:T(4,128)(2,1)S(1)}, u32[]{:S(2)}, u32[]{:S(2)}) collective-permute-start(bf16[4,2048]{1,0:T(4,128)(2,1)S(1)} %maximum_select_fusion.3), channel_id=1, source_target_pairs={{0,8},{4,12},{8,0},{12,4},{16,24},{20,28},{24,16},{28,20},{1,9},{5... | collective-permute-start | bytes 49160 | tf_op jit(solution)/shard_map/ppermute | solution.py:14
  250.2 5.2 %collective-permute-start.2 = (bf16[8,2048]{1,0:T(8,128)(2,1)S(1)}, bf16[8,2048]{1,0:T(8,128)(2,1)S(1)}, u32[]{:S(2)}, u32[]{:S(2)}) collective-permute-start(bf16[8,2048]{1,0:T(8,128)(2,1)S(1)} %maximum_select_fusion.1), channel_id=1, source_target_pairs={{0,16},{4,20},{8,24},{12,28},{16,0},{20,4},{24,8},{28,12},{1,17},{... | collective-permute-start | bytes 98312 | tf_op jit(solution)/shard_map/ppermute | solution.py:14
  256.1 3.7 %collective-permute-start.15 = (f32[16,16]{1,0:T(8,128)S(1)}, f32[16,16]{1,0:T(8,128)S(1)}, u32[]{:S(2)}, u32[]{:S(2)}) collective-permute-start(f32[16,16]{1,0:T(8,128)S(1)} %copy.359), channel_id=1, source_target_pairs={{0,4},{4,0},{8,12},{12,8},{16,20},{20,16},{24,28},{28,24},{1,5},{5... | collective-permute-start | bytes 3080 | tf_op jit(solution)/shard_map/ppermute | solution.py:14
  256.5 3.7 %collective-permute-start.3 = (f32[16,16]{1,0:T(8,128)S(1)}, f32[16,16]{1,0:T(8,128)S(1)}, u32[]{:S(2)}, u32[]{:S(2)}) collective-permute-start(f32[16,16]{1,0:T(8,128)S(1)} %copy.340), channel_id=1, source_target_pairs={{0,4},{4,0},{8,12},{12,8},{16,20},{20,16},{24,28},{28,24},{1,5},{5... | collective-permute-start | bytes 3080 | tf_op jit(solution)/shard_map/ppermute | solution.py:14
  260.2 3.7 %collective-permute-start.16 = (f32[16,16]{1,0:T(8,128)S(1)}, f32[16,16]{1,0:T(8,128)S(1)}, u32[]{:S(2)}, u32[]{:S(2)}) collective-permute-start(f32[16,16]{1,0:T(8,128)S(1)} %get-tuple-element.38), channel_id=1, source_target_pairs={{0,8},{4,12},{8,0},{12,4},{16,24},{20,28},{24,16},{28,20},{1,9},{5... | collective-permute-start | bytes 3080 | tf_op jit(solution)/shard_map/ppermute | solution.py:14
  260.7 3.7 %collective-permute-start.5 = (f32[16,16]{1,0:T(8,128)S(1)}, f32[16,16]{1,0:T(8,128)S(1)}, u32[]{:S(2)}, u32[]{:S(2)}) collective-permute-start(f32[16,16]{1,0:T(8,128)S(1)} %get-tuple-element.41), channel_id=1, source_target_pairs={{0,8},{4,12},{8,0},{12,4},{16,24},{20,28},{24,16},{28,20},{1,9},{5... | collective-permute-start | bytes 3080 | tf_op jit(solution)/shard_map/ppermute | solution.py:14
  264.3 5.4 %collective-permute-start.7 = (f32[16,16]{1,0:T(8,128)S(1)}, f32[16,16]{1,0:T(8,128)S(1)}, u32[]{:S(2)}, u32[]{:S(2)}) collective-permute-start(f32[16,16]{1,0:T(8,128)S(1)} %get-tuple-element.37), channel_id=1, source_target_pairs={{0,16},{4,20},{8,24},{12,28},{16,0},{20,4},{24,8},{28,12},{1,17},{... | collective-permute-start | bytes 3080 | tf_op jit(solution)/shard_map/ppermute | solution.py:14
  267.1 5.0 %collective-permute-start.4 = (f32[16,16,128]{2,1,0:T(8,128)S(1)}, f32[16,16,128]{2,1,0:T(8,128)S(1)}, u32[]{:S(2)}, u32[]{:S(2)}) collective-permute-start(f32[16,16,128]{2,1,0:T(8,128)S(1)} %copy.341), channel_id=1, source_target_pairs={{0,4},{4,0},{8,12},{12,8},{16,20},{20,16},{24,28},{28,24},{1,5},{5... | collective-permute-start | bytes 393224 | tf_op jit(solution)/shard_map/ppermute | solution.py:14
  267.6 10.5 %collective-permute-start.17 = (f32[16,16]{1,0:T(8,128)S(1)}, f32[16,16]{1,0:T(8,128)S(1)}, u32[]{:S(2)}, u32[]{:S(2)}) collective-permute-start(f32[16,16]{1,0:T(8,128)S(1)} %get-tuple-element.25), channel_id=1, source_target_pairs={{0,16},{4,20},{8,24},{12,28},{16,0},{20,4},{24,8},{28,12},{1,17},{... | collective-permute-start | bytes 3080 | tf_op jit(solution)/shard_map/ppermute | solution.py:14
  272.3 5.0 %collective-permute-start.6 = (f32[16,16,128]{2,1,0:T(8,128)S(1)}, f32[16,16,128]{2,1,0:T(8,128)S(1)}, u32[]{:S(2)}, u32[]{:S(2)}) collective-permute-start(f32[16,16,128]{2,1,0:T(8,128)S(1)} %multiply_add_fusion.1), channel_id=1, source_target_pairs={{0,8},{4,12},{8,0},{12,4},{16,24},{20,28},{24,16},{28,20},{1,9},{5... | collective-permute-start | bytes 393224 | tf_op jit(solution)/shard_map/ppermute | solution.py:14
  277.5 7.3 %collective-permute-start.8 = (f32[16,16,128]{2,1,0:T(8,128)S(1)}, f32[16,16,128]{2,1,0:T(8,128)S(1)}, u32[]{:S(2)}, u32[]{:S(2)}) collective-permute-start(f32[16,16,128]{2,1,0:T(8,128)S(1)} %multiply_add_fusion), channel_id=1, source_target_pairs={{0,16},{4,20},{8,24},{12,28},{16,0},{20,4},{24,8},{28,12},{1,17},{... | collective-permute-start | bytes 393224 | tf_op jit(solution)/shard_map/ppermute | solution.py:14
Sparse Core Ops, SparseCore 0:
  144.4 29.3 all-reduce.3
where the time goes:
time: 293 us; the launch traced here: 292 us
  blocking collectives  157 us (54%)
  waiting for transfers between devices  73.7 us (25%)
  starting transfers between devices  27.3 us (9%)
  between operations  15.8 us (5%)
  matrix products  10.7 us (4%)
  local copies, waits for them, and re-layouts  4.32 us (1%)
  other arithmetic  3.5 us (1%)
    unnamed x1, blocking collectives  34.8 us
    ppermute x18, waiting for transfers between devices, swapped(): lax.ppermute(array, axis, [(i, i ^ 1 << apart) for i in range(lax.axis_si...  32.9 us
    all_gather x1, blocking collectives, shards(): lax.all_gather(query_low, 'seq', axis=0, tiled=True)  32.6 us
    all_gather x1, blocking collectives, shards(): lower_all = lax.all_gather(own_heads, 'seq', axis=0, tiled=True)  30.6 us
    psum x1, waiting for transfers between devices, shards(): summed = lax.psum(head_terms, 'tp')  28.2 us
    psum x1, blocking collectives, shards(): squares = lax.psum(jnp.sum(residual * residual, axis=1), 'seq')  21.4 us
    all_gather x1, blocking collectives, shards(): lax.all_gather(key_tree_low, 'seq', axis=0, tiled=True)  21.2 us
    all_gather x1, blocking collectives, shards(): lax.all_gather(value_tree_low, 'seq', axis=0, tiled=True)  16.6 us
  transfers between devices with their start and end apart: 22, of which 17 were waited for; matrix products, arithmetic and copies ran while one was open for 3% of the time, Pallas kernels for 0%

commit v1 on v0

v1 whole, which is shorter than its diff:
```python
import functools

import jax
import jax.numpy as jnp
from jax import lax
from jax.experimental import pallas as pl
from jax.experimental.pallas import tpu as pltpu
from jax.sharding import PartitionSpec as P

MESH = pl.DeviceIdType.MESH
F32 = jnp.float32
BF16 = jnp.bfloat16
masked_score = -1e30
lowest_high = -1e29
norm_epsilon = 1e-05


def attend(queries, keys, values, allowed, scale):
    scores = lax.dot_general(
        queries, keys, (((1,), (1,)), ((), ())), preferred_element_type=F32
    ) * scale
    scores = jnp.where(allowed, scores, masked_score)
    high = jnp.maximum(jnp.max(scores, axis=1, keepdims=True), lowest_high)
    weights = jnp.exp(scores - high)
    total = jnp.sum(weights, axis=1, keepdims=True)
    blend = jnp.dot(weights.astype(BF16), values, preferred_element_type=F32)
    return blend, high, total


def kernel(
    sizes,
    lens_ref,
    q_ref,
    k_ref,
    v_ref,
    hid_ref,
    anc_ref,
    gain_ref,
    ridx_ref,
    ck_hbm,
    cv_hbm,
    ow_hbm,
    wk_hbm,
    wv_hbm,
    wq_hbm,
    rk_hbm,
    rv_hbm,
    res_ref,
    up_ref,
    ck,
    cv,
    ow,
    wk,
    wv,
    wq,
    rk,
    rv,
    form,
    low,
    part,
    stat,
    gpart,
    gstat,
    heads,
    terms,
    proj,
    gproj,
    upper,
    upart,
    ustat,
    ugpart,
    ugstat,
    load_sem,
    send_sem,
    recv_sem,
):
    S, T, R, own, kv, g, hd = sizes
    G = S // R
    M = S * own
    rows = own * g
    nodes = G * own
    scale = hd ** (-0.5)
    width = S * hid_ref.shape[1]
    me = lax.axis_index("seq")
    tp = lax.axis_index("tp")
    request = me // G
    base = request * G
    place = me - base

    barrier = pltpu.get_barrier_semaphore()
    for d in range(1, S):
        pl.semaphore_signal(
            barrier, inc=1, device_id={"seq": lax.rem(me + d, S)}, device_id_type=MESH
        )
    for d in range(1, T):
        pl.semaphore_signal(
            barrier, inc=1, device_id={"tp": lax.rem(tp + d, T)}, device_id_type=MESH
        )

    loads = []
    for i, (src, dst) in enumerate(
        (
            (ck_hbm, ck),
            (cv_hbm, cv),
            (ow_hbm, ow),
            (wk_hbm, wk),
            (wv_hbm, wv),
            (wq_hbm, wq),
            (rk_hbm, rk),
            (rv_hbm, rv),
        )
    ):
        copy = pltpu.make_async_copy(src, dst, load_sem.at[i])
        copy.start()
        loads.append(copy)

    sent = []

    def send(phase, d, src, dst, target):
        copy = pltpu.make_async_remote_copy(
            src_ref=src,
            dst_ref=dst,
            send_sem=send_sem.at[phase, d],
            recv_sem=recv_sem.at[phase, d],
            device_id=target,
            device_id_type=MESH,
        )
        copy.start()
        sent.append(copy)

    def arrive(phase, d, src, dst, target):
        pltpu.make_async_remote_copy(
            src_ref=src,
            dst_ref=dst,
            send_sem=send_sem.at[phase, d],
            recv_sem=recv_sem.at[phase, d],
            device_id=target,
            device_id_type=MESH,
        ).wait_recv()

    def peer(d):
        return lax.rem(me + d, S)

    def mate(d):
        return lax.rem(place + d, G)

    def spread(count, first, value):
        return value

    def tree_rows(block, j):
        return block[pl.ds(j, nodes, stride=g), :].astype(BF16)

    mask_rows = []
    node_start = place * own
    for r in range(own):
        row = anc_ref[request, pl.ds(node_start + r, 1), :]
        mask_rows.append(jnp.broadcast_to(row, (g, nodes)))
    tree_mask = jnp.concatenate(mask_rows, axis=0) > 0

    lanes = lax.broadcasted_iota(jnp.int32, (nodes * g, hd), 1)

    def pack_stats(stats):
        packed = jnp.zeros((nodes * g, hd), F32)
        for k, (high, total) in enumerate(stats):
            packed = jnp.where(lanes == 2 * k, high, packed)
            packed = jnp.where(lanes == 2 * k + 1, total, packed)
        return packed

    def finish(stats_ref, parts_ref, count, own_queries, tree_block):
        stats = [stats_ref[s] for s in range(count)]
        top = functools.reduce(jnp.maximum, stats)
        factors = [jnp.exp(x - top) for x in stats]
        done = []
        for k in range(kv):
            blend, high, total = attend(
                own_queries[k],
                tree_rows(tree_block, k),
                tree_rows(tree_block, kv + k),
                tree_mask,
                scale,
            )
            part_top = top[:, 2 * k : 2 * k + 1]
            highest = jnp.maximum(part_top, high)
            late = jnp.exp(high - highest)
            early = jnp.exp(part_top - highest)
            acc = jnp.zeros((rows, hd), F32)
            mass = jnp.zeros((rows, 1), F32)
            for s in range(count):
                factor = factors[s][:, 2 * k : 2 * k + 1]
                acc = acc + parts_ref[s, k].astype(F32) * factor
                mass = mass + stats[s][:, 2 * k + 1 : 2 * k + 2] * factor
            done.append((acc * early + blend * late) / (mass * early + total * late))
        return done

    form[kv] = jnp.zeros((M * g, hd), F32)
    q_rows = q_ref[...].astype(F32)
    k_rows = k_ref[...].astype(F32)
    v_rows = v_ref[...].astype(F32)
    for k in range(kv):
        for j in range(g):
            h = k * g + j
            form[k, pl.ds(j, own, stride=g), :] = q_rows[:, h * hd : (h + 1) * hd]
        form[kv, pl.ds(k, own, stride=g), :] = k_rows[:, k * hd : (k + 1) * hd]
        form[kv, pl.ds(kv + k, own, stride=g), :] = v_rows[:, k * hd : (k + 1) * hd]
    for k in range(kv + 1):
        low[me, k] = form[k, :rows, :].astype(BF16)

    pl.semaphore_wait(barrier, S - 1 + T - 1)

    for d in range(1, S):
        send(0, d, low.at[me], low.at[me], {"seq": peer(d)})
    loads[0].wait()
    loads[1].wait()
    for d in range(1, S):
        source = peer(S - d)
        arrive(0, d, low.at[source], low.at[source], {"seq": source})

    columns = ck.shape[1]
    column = lax.broadcasted_iota(jnp.int32, (1, columns), 1)
    first = me * (columns // kv)

    def cache_request(r, carry):
        limit = (lens_ref[r] - first) * kv
        stats = []
        for k in range(kv):
            queries = low[pl.ds(r * G, G), k].reshape(nodes * g, hd)
            allowed = jnp.logical_and(
                jnp.bitwise_and(column, kv - 1) == k, column < limit
            )
            blend, high, total = attend(queries, ck[r], cv[r], allowed, scale)
            stats.append((high, total))
            for a in range(G):
                part[r * G + a, k] = blend[a * rows : (a + 1) * rows].astype(BF16)
        packed = pack_stats(stats)
        for a in range(G):
            stat[r * G + a] = packed[a * rows : (a + 1) * rows]
        return carry

    if R == 1:
        cache_request(0, 0)
    else:
        lax.fori_loop(0, R, cache_request, 0)
    for d in range(1, S):
        target = peer(d)
        send(1, d, part.at[target], gpart.at[me], {"seq": target})
        send(2, d, stat.at[target], gstat.at[me], {"seq": target})
    gpart[me] = part[me]
    gstat[me] = stat[me]
    form[kv, : nodes * g, :] = low[pl.ds(base, G), kv].reshape(nodes * g, hd).astype(F32)
    own_queries = [low[me, k] for k in range(kv)]
    for d in range(1, S):
        source = peer(S - d)
        arrive(1, d, part.at[source], gpart.at[source], {"seq": source})
        arrive(2, d, stat.at[source], gstat.at[source], {"seq": source})

    done = finish(gstat, gpart, S, own_queries, form.at[kv])
    for k in range(kv):
        heads[me, k] = done[k].astype(BF16)
    for d in range(1, S):
        send(3, d, heads.at[me], heads.at[me], {"seq": peer(d)})
    loads[2].wait()
    for d in range(1, S):
        source = peer(S - d)
        arrive(3, d, heads.at[source], heads.at[source], {"seq": source})

    for k in range(kv):
        form[k] = heads[:, k].reshape(M * g, hd).astype(F32)
    lower = jnp.concatenate(
        [
            form[k, pl.ds(j, M, stride=g), :].astype(BF16)
            for k in range(kv)
            for j in range(g)
        ],
        axis=1,
    )
    terms[tp] = jnp.dot(lower, ow[...], preferred_element_type=F32).astype(BF16)
    for d in range(1, T):
        send(4, d, terms.at[tp], terms.at[tp], {"tp": lax.rem(tp + d, T)})
    loads[3].wait()
    loads[4].wait()
    loads[5].wait()
    for d in range(1, T):
        source = lax.rem(tp + T - d, T)
        arrive(4, d, terms.at[source], terms.at[source], {"tp": source})
    residual = hid_ref[...].astype(F32)
    summed = terms[0].astype(F32)
    for t in range(1, T):
        summed = summed + terms[t].astype(F32)
    residual = residual + summed
    res_ref[...] = residual

    squares = jnp.broadcast_to(jnp.sum(residual * residual, axis=1, keepdims=True), (M, hd))
    coarse = squares.astype(BF16).astype(F32)
    scaled = (residual * gain_ref[...]).astype(BF16)
    query_terms = jnp.dot(scaled, wq[...], preferred_element_type=F32)
    key_terms = jnp.dot(scaled, wk[...], preferred_element_type=F32)
    value_terms = jnp.dot(scaled, wv[...], preferred_element_type=F32)
    form[kv] = jnp.zeros((M * g, hd), F32)
    for k in range(kv):
        for j in range(g):
            h = k * g + j
            form[k, pl.ds(j, M, stride=g), :] = query_terms[:, h * hd : (h + 1) * hd]
        form[kv, pl.ds(k, M, stride=g), :] = key_terms[:, k * hd : (k + 1) * hd]
        form[kv, pl.ds(kv + k, M, stride=g), :] = value_terms[:, k * hd : (k + 1) * hd]
    form[kv, pl.ds(2 * kv, M, stride=g), :] = coarse
    form[kv, pl.ds(2 * kv + 1, M, stride=g), :] = squares - coarse
    for s in range(S):
        for k in range(kv + 1):
            proj[s, k] = form[k, s * rows : (s + 1) * rows, :].astype(BF16)
    for d in range(1, S):
        target = peer(d)
        send(5, d, proj.at[target], gproj.at[me], {"seq": target})
    gproj[me] = proj[me]
    for d in range(1, S):
        source = peer(S - d)
        arrive(5, d, proj.at[source], gproj.at[source], {"seq": source})
    sums = []
    for k in range(kv + 1):
        total = gproj[0, k].astype(F32)
        for s in range(1, S):
            total = total + gproj[s, k].astype(F32)
        sums.append(total)
    inverses = []
    for r in range(own):
        at = r * g + 2 * kv
        square = sums[kv][at : at + 1, :] + sums[kv][at + 1 : at + 2, :]
        inverse = lax.rsqrt(square / width + norm_epsilon)
        inverses.append(jnp.broadcast_to(inverse, (g, hd)))
    inverse = jnp.concatenate(inverses, axis=0)

    own_queries = []
    for k in range(kv + 1):
        block = (sums[k] * inverse).astype(BF16)
        upper[place, k] = block
        own_queries.append(block)
    for d in range(1, G):
        send(6, d, upper.at[place], upper.at[place], {"seq": base + mate(d)})
    loads[6].wait()
    loads[7].wait()
    for d in range(1, G):
        source = mate(G - d)
        arrive(6, d, upper.at[source], upper.at[source], {"seq": base + source})

    entries = rk.shape[0]
    entry = lax.broadcasted_iota(jnp.int32, (1, entries), 1)
    kept = ridx_ref[...] < lens_ref[request]
    stats = []
    for k in range(kv):
        allowed = jnp.logical_and(jnp.bitwise_and(entry, kv - 1) == k, kept)
        queries = upper[:, k].reshape(nodes * g, hd)
        blend, high, total = attend(queries, rk[...], rv[...], allowed, scale)
        stats.append((high, total))
        for a in range(G):
            upart[a, k] = blend[a * rows : (a + 1) * rows].astype(BF16)
    packed = pack_stats(stats)
    for a in range(G):
        ustat[a] = packed[a * rows : (a + 1) * rows]
    for d in range(1, G):
        target = mate(d)
        send(7, d, upart.at[target], ugpart.at[place], {"seq": base + target})
        send(8, d, ustat.at[target], ugstat.at[place], {"seq": base + target})
    ugpart[place] = upart[place]
    ugstat[place] = ustat[place]
    form[kv, : nodes * g, :] = upper[:, kv].reshape(nodes * g, hd).astype(F32)
    for d in range(1, G):
        source = mate(G - d)
        arrive(7, d, upart.at[source], ugpart.at[source], {"seq": base + source})
        arrive(8, d, ustat.at[source], ugstat.at[source], {"seq": base + source})
    done = finish(ugstat, ugpart, G, own_queries, form.at[kv])
    for k in range(kv):
        form[k, :rows, :] = done[k]
        for j in range(g):
            h = k * g + j
            up_ref[:, h * hd : (h + 1) * hd] = form[k, pl.ds(j, own, stride=g), :]
    for copy in sent:
        copy.wait_send()


def shards(
    tree_hidden,
    query_low,
    key_tree_low,
    value_tree_low,
    cache_keys,
    cache_values,
    cache_lengths,
    ancestors,
    out_weight,
    norm_gain,
    w_query_up,
    w_key_up,
    w_value_up,
    retained_keys,
    retained_values,
    retained_index,
):
    S = lax.axis_size("seq")
    T = lax.axis_size("tp")
    R, part, kv, hd = cache_keys.shape
    own, row_width = query_low.shape
    g = row_width // (kv * hd)
    G = S // R
    M = S * own
    rows = own * g
    features = tree_hidden.shape[1]
    entries = retained_keys.shape[1] * kv
    ck = cache_keys.reshape(R, part * kv, hd)
    cv = cache_values.reshape(R, part * kv, hd)
    rk = retained_keys.reshape(entries, hd)
    rv = retained_values.reshape(entries, hd)
    ridx = retained_index.reshape(1, entries)
    gain = norm_gain.reshape(1, features)
    vmem = pl.BlockSpec(memory_space=pltpu.VMEM)
    hbm = pl.BlockSpec(memory_space=pl.ANY)
    big = (ck, cv, out_weight, w_key_up, w_value_up, w_query_up, rk, rv)
    return pl.pallas_call(
        functools.partial(kernel, (S, T, R, own, kv, g, hd)),
        out_shape=(
            jax.ShapeDtypeStruct((M, features), F32),
            jax.ShapeDtypeStruct((own, row_width), F32),
        ),
        in_specs=[pl.BlockSpec(memory_space=pltpu.SMEM)] + [vmem] * 7 + [hbm] * 8,
        out_specs=(vmem, vmem),
        scratch_shapes=[pltpu.VMEM(x.shape, x.dtype) for x in big]
        + [
            pltpu.VMEM((kv + 1, M * g, hd), F32),
            pltpu.VMEM((S, kv + 1, rows, hd), BF16),
            pltpu.VMEM((S, kv, rows, hd), BF16),
            pltpu.VMEM((S, rows, hd), F32),
            pltpu.VMEM((S, kv, rows, hd), BF16),
            pltpu.VMEM((S, rows, hd), F32),
            pltpu.VMEM((S, kv, rows, hd), BF16),
            pltpu.VMEM((T, M, features), BF16),
            pltpu.VMEM((S, kv + 1, rows, hd), BF16),
            pltpu.VMEM((S, kv + 1, rows, hd), BF16),
            pltpu.VMEM((G, kv + 1, rows, hd), BF16),
            pltpu.VMEM((G, kv, rows, hd), BF16),
            pltpu.VMEM((G, rows, hd), F32),
            pltpu.VMEM((G, kv, rows, hd), BF16),
            pltpu.VMEM((G, rows, hd), F32),
            pltpu.SemaphoreType.DMA((len(big),)),
            pltpu.SemaphoreType.DMA((9, max(S, T))),
            pltpu.SemaphoreType.DMA((9, max(S, T))),
        ],
        compiler_params=pltpu.CompilerParams(
            collective_id=0, has_side_effects=True, vmem_limit_bytes=56 * 1024 * 1024
        ),
        name="two_layers",
    )(
        cache_lengths,
        query_low,
        key_tree_low,
        value_tree_low,
        tree_hidden,
        ancestors,
        gain,
        ridx,
        *big,
    )


def solution(mesh):
    return jax.shard_map(
        shards,
        mesh=mesh,
        in_specs=(
            P(None, "seq"),
            P("seq", "tp"),
            P("seq", "tp"),
            P("seq", "tp"),
            P(None, "seq", "tp", None),
            P(None, "seq", "tp", None),
            P(),
            P(),
            P("tp", "seq"),
            P("seq"),
            P("seq", "tp"),
            P("seq", "tp"),
            P("seq", "tp"),
            P("seq", None, "tp", None),
            P("seq", None, "tp", None),
            P("seq", None, "tp"),
        ),
        out_specs=(P(None, "seq"), P("seq", "tp")),
        check_vma=False,
    )
```

time: 293 us -> 49 us (0.17)
  blocking collectives: 157 us -> 0 us
  waiting for transfers between devices: 73.7 us -> 0 us
  Pallas kernels: 0 us -> 43 us
  starting transfers between devices: 27.3 us -> 0 us
  between operations: 15.8 us -> 1.3 us
  matrix products: 10.7 us -> 0 us
  other arithmetic: 3.5 us -> 0 us
    all_gather x4 -> x0, blocking collectives: 101 us -> none  [the longest x1 32.6 us: shards(): lax.all_gather(query_low, 'seq', axis=0, tiled=True)]
    pallas_call x0 -> x1, Pallas kernels: none -> 43 us  [shards(): pl.pallas_call(functools.partial(kernel, (S, T, R, own, kv, g, hd)), out_...]
    unnamed x1 -> x0, blocking collectives: 34.8 us -> none
    ppermute x18 -> x0, waiting for transfers between devices: 32.9 us -> none  [swapped(): lax.ppermute(array, axis, [(i, i ^ 1 << apart) for i in range(lax.axis_si...]
    psum x1 -> x0, waiting for transfers between devices: 28.2 us -> none  [shards(): summed = lax.psum(head_terms, 'tp')]
    psum x1 -> x0, blocking collectives: 21.4 us -> none  [shards(): squares = lax.psum(jnp.sum(residual * residual, axis=1), 'seq')]
    ppermute x18 -> x0, starting transfers between devices: 15.1 us -> none  [swapped(): lax.ppermute(array, axis, [(i, i ^ 1 << apart) for i in range(lax.axis_si...]
    all_to_all x3 -> x0, waiting for transfers between devices: 12.6 us -> none  [the longest x1 7.11 us: shards(): lax.all_to_all(part_blend[None], 'seq', split_axis=1, concat_axis=0, tile...]
  transfers between devices with their start and end apart: 22 -> 0, of which waited for: 17 -> 0; matrix products, arithmetic and copies ran while one was open for 3% -> 0% of each run, Pallas kernels for 0% -> 0%
where the time goes in v1:
time: 49 us; the launch traced here: 48.7 us
  Pallas kernels  43 us (88%)
  local copies, waits for them, and re-layouts  4.4 us (9%)
  between operations  1.3 us (3%)
    pallas_call x1, Pallas kernels, shards(): pl.pallas_call(functools.partial(kernel, (S, T, R, own, kv, g, hd)), out_...  43 us
    unnamed x3, local copies, waits for them, and re-layouts  3.62 us

profile of v1, /device:TPU:0, one launch (start us, length us, event | category | flops | bytes accessed | tf_op | source)
XLA Modules:
  0.0 48.7 jit_solution(4691087189299164368)
XLA Ops:
  0.6 0.8 %copy.19 = s32[1,512,2]{2,1,0:T(8,128)S(1)} copy(s32[1,512,2]{1,2,0:T(2,128)} %param.31) | data formatting | bytes 8192 | tf_op args[15]
  1.5 0.8 %reshape.23.ridx_ref = s32[1,1024]{1,0:T(1,128)} reshape(s32[1,512,2]{2,1,0:T(8,128)S(1)} %copy.19) | data formatting | bytes 8192 | tf_op jit(solution)/shard_map/reshape | solution.py:411
  2.9 43.0 %two_layers.1 = (f32[16,1024]{1,0:T(8,128)}, f32[2,2048]{1,0:T(2,128)}) custom-call(s32[1]{0:T(128)S(6)} %copy.22.lens_ref, bf16[2,2048]{1,0:T(2,128)(2,1)} %q_ref.1, bf16[2,256]{1,0:T(2,128)(2,1)} %k_ref.1, bf16[2,256]{1,0:T(2,128)(2,1)} %v_ref.1, bf16[16,1024]{1,0:T(8,128)(2,1)} %hid_ref.1, s32[1,16,16]{2,1,0:T(8,128)} %anc_ref.1, f32[1,1024]{1,0:T(1,128)} %bitcast.9, ...), custom_call_target="tpu_custom_call" | custom-call | tf_op jit(solution)/shard_map/two_layers/pallas_call | solution.py:416
  45.9 1.5 %copy.23 = f32[16,1024]{1,0:T(8,128)} copy(f32[16,1024]{1,0:T(8,128)} %get-tuple-element.4) | data formatting | bytes 131072
  47.3 1.3 %copy.24 = f32[2,2048]{1,0:T(2,128)} copy(f32[2,2048]{1,0:T(2,128)} %get-tuple-element.5) | data formatting | bytes 32768

commit v2 on v1

--- a/solution.py
+++ b/solution.py
@@ -29,47 +29,51 @@
 
 def kernel(
     sizes,
+    lens_hbm,
+    q_hbm,
+    k_hbm,
+    v_hbm,
+    ck_hbm,
+    cv_hbm,
+    anc_hbm,
+    ow_hbm,
+    hid_hbm,
+    gain_hbm,
+    wk_hbm,
+    wv_hbm,
+    wq_hbm,
+    ridx_hbm,
+    rk_hbm,
+    rv_hbm,
+    res_ref,
+    up_ref,
     lens_ref,
     q_ref,
     k_ref,
     v_ref,
-    hid_ref,
-    anc_ref,
-    gain_ref,
-    ridx_ref,
-    ck_hbm,
-    cv_hbm,
-    ow_hbm,
-    wk_hbm,
-    wv_hbm,
-    wq_hbm,
-    rk_hbm,
-    rv_hbm,
-    res_ref,
-    up_ref,
     ck,
     cv,
+    anc_ref,
     ow,
+    hid_ref,
+    gain_ref,
     wk,
     wv,
     wq,
+    ridx_ref,
     rk,
     rv,
     form,
     low,
     part,
-    stat,
     gpart,
-    gstat,
     heads,
     terms,
     proj,
     gproj,
     upper,
     upart,
-    ustat,
     ugpart,
-    ugstat,
     load_sem,
     send_sem,
     recv_sem,
@@ -100,14 +104,22 @@
     loads = []
     for i, (src, dst) in enumerate(
         (
+            (q_hbm, q_ref),
+            (k_hbm, k_ref),
+            (v_hbm, v_ref),
             (ck_hbm, ck),
             (cv_hbm, cv),
+            (anc_hbm, anc_ref),
             (ow_hbm, ow),
+            (hid_hbm, hid_ref),
+            (gain_hbm, gain_ref),
             (wk_hbm, wk),
             (wv_hbm, wv),
             (wq_hbm, wq),
+            (ridx_hbm, ridx_ref),
             (rk_hbm, rk),
             (rv_hbm, rv),
+            (lens_hbm, lens_ref),
         )
     ):
         copy = pltpu.make_async_copy(src, dst, load_sem.at[i])
@@ -144,41 +156,49 @@
     def mate(d):
         return lax.rem(place + d, G)
 
-    def spread(count, first, value):
-        return value
-
     def tree_rows(block, j):
         return block[pl.ds(j, nodes, stride=g), :].astype(BF16)
 
-    mask_rows = []
-    node_start = place * own
-    for r in range(own):
-        row = anc_ref[request, pl.ds(node_start + r, 1), :]
-        mask_rows.append(jnp.broadcast_to(row, (g, nodes)))
-    tree_mask = jnp.concatenate(mask_rows, axis=0) > 0
-
     lanes = lax.broadcasted_iota(jnp.int32, (nodes * g, hd), 1)
+
+    third = 32
 
     def pack_stats(stats):
         packed = jnp.zeros((nodes * g, hd), F32)
+        spot = jnp.bitwise_and(lanes, third - 1)
         for k, (high, total) in enumerate(stats):
-            packed = jnp.where(lanes == 2 * k, high, packed)
-            packed = jnp.where(lanes == 2 * k + 1, total, packed)
-        return packed
-
-    def finish(stats_ref, parts_ref, count, own_queries, tree_block):
-        stats = [stats_ref[s] for s in range(count)]
-        top = functools.reduce(jnp.maximum, stats)
-        factors = [jnp.exp(x - top) for x in stats]
-        done = []
-        for k in range(kv):
-            blend, high, total = attend(
+            packed = jnp.where(spot == 2 * k, high, packed)
+            packed = jnp.where(spot == 2 * k + 1, total, packed)
+        coarse = packed.astype(BF16).astype(F32)
+        rest = packed - coarse
+        middle = rest.astype(BF16).astype(F32)
+        fine = rest - middle
+        packed = jnp.where(lanes < third, coarse, jnp.where(lanes < 2 * third, middle, fine))
+        return jnp.where(lanes < 3 * third, packed, 0.0).astype(BF16)
+
+    def unpack_stats(block):
+        packed = block.astype(F32)
+        return (packed + pltpu.roll(packed, hd - third, 1)) + pltpu.roll(packed, hd - 2 * third, 1)
+
+    def tree_part(own_queries, tree_block, tree_mask):
+        return [
+            attend(
                 own_queries[k],
                 tree_rows(tree_block, k),
                 tree_rows(tree_block, kv + k),
                 tree_mask,
                 scale,
             )
+            for k in range(kv)
+        ]
+
+    def finish(parts_ref, count, trees):
+        stats = [unpack_stats(parts_ref[s, kv]) for s in range(count)]
+        top = functools.reduce(jnp.maximum, stats)
+        factors = [jnp.exp(x - top) for x in stats]
+        done = []
+        for k in range(kv):
+            blend, high, total = trees[k]
             part_top = top[:, 2 * k : 2 * k + 1]
             highest = jnp.maximum(part_top, high)
             late = jnp.exp(high - highest)
@@ -193,6 +213,8 @@
         return done
 
     form[kv] = jnp.zeros((M * g, hd), F32)
+    for i in range(3):
+        loads[i].wait()
     q_rows = q_ref[...].astype(F32)
     k_rows = k_ref[...].astype(F32)
     v_rows = v_ref[...].astype(F32)
@@ -208,12 +230,25 @@
     pl.semaphore_wait(barrier, S - 1 + T - 1)
 
     for d in range(1, S):
-        send(0, d, low.at[me], low.at[me], {"seq": peer(d)})
-    loads[0].wait()
-    loads[1].wait()
+        own_q = low.at[me, pl.ds(0, kv)]
+        send(0, d, own_q, own_q, {"seq": peer(d)})
+    for d in range(1, S):
+        own_kv = low.at[me, pl.ds(kv, 1)]
+        send(2, d, own_kv, own_kv, {"seq": peer(d)})
+    loads[3].wait()
+    loads[4].wait()
+    loads[5].wait()
+    loads[15].wait()
+    mask_rows = []
+    node_start = place * own
+    for r in range(own):
+        row = anc_ref[request, pl.ds(node_start + r, 1), :]
+        mask_rows.append(jnp.broadcast_to(row, (g, nodes)))
+    tree_mask = jnp.concatenate(mask_rows, axis=0) > 0
     for d in range(1, S):
         source = peer(S - d)
-        arrive(0, d, low.at[source], low.at[source], {"seq": source})
+        there = low.at[source, pl.ds(0, kv)]
+        arrive(0, d, there, there, {"seq": source})
 
     columns = ck.shape[1]
     column = lax.broadcasted_iota(jnp.int32, (1, columns), 1)
@@ -233,7 +268,7 @@
                 part[r * G + a, k] = blend[a * rows : (a + 1) * rows].astype(BF16)
         packed = pack_stats(stats)
         for a in range(G):
-            stat[r * G + a] = packed[a * rows : (a + 1) * rows]
+            part[r * G + a, kv] = packed[a * rows : (a + 1) * rows]
         return carry
 
     if R == 1:
@@ -243,22 +278,23 @@
     for d in range(1, S):
         target = peer(d)
         send(1, d, part.at[target], gpart.at[me], {"seq": target})
-        send(2, d, stat.at[target], gstat.at[me], {"seq": target})
     gpart[me] = part[me]
-    gstat[me] = stat[me]
+    for d in range(1, S):
+        source = peer(S - d)
+        there = low.at[source, pl.ds(kv, 1)]
+        arrive(2, d, there, there, {"seq": source})
     form[kv, : nodes * g, :] = low[pl.ds(base, G), kv].reshape(nodes * g, hd).astype(F32)
-    own_queries = [low[me, k] for k in range(kv)]
+    trees = tree_part([low[me, k] for k in range(kv)], form.at[kv], tree_mask)
     for d in range(1, S):
         source = peer(S - d)
         arrive(1, d, part.at[source], gpart.at[source], {"seq": source})
-        arrive(2, d, stat.at[source], gstat.at[source], {"seq": source})
-
-    done = finish(gstat, gpart, S, own_queries, form.at[kv])
+
+    done = finish(gpart, S, trees)
     for k in range(kv):
         heads[me, k] = done[k].astype(BF16)
     for d in range(1, S):
         send(3, d, heads.at[me], heads.at[me], {"seq": peer(d)})
-    loads[2].wait()
+    loads[6].wait()
     for d in range(1, S):
         source = peer(S - d)
         arrive(3, d, heads.at[source], heads.at[source], {"seq": source})
@@ -276,9 +312,8 @@
     terms[tp] = jnp.dot(lower, ow[...], preferred_element_type=F32).astype(BF16)
     for d in range(1, T):
         send(4, d, terms.at[tp], terms.at[tp], {"tp": lax.rem(tp + d, T)})
-    loads[3].wait()
-    loads[4].wait()
-    loads[5].wait()
+    for i in range(7, 12):
+        loads[i].wait()
     for d in range(1, T):
         source = lax.rem(tp + T - d, T)
         arrive(4, d, terms.at[source], terms.at[source], {"tp": source})
@@ -334,19 +369,36 @@
         upper[place, k] = block
         own_queries.append(block)
     for d in range(1, G):
-        send(6, d, upper.at[place], upper.at[place], {"seq": base + mate(d)})
-    loads[6].wait()
-    loads[7].wait()
+        own_q = upper.at[place, pl.ds(0, kv)]
+        send(6, d, own_q, own_q, {"seq": base + mate(d)})
+    for d in range(1, G):
+        own_kv = upper.at[place, pl.ds(kv, 1)]
+        send(8, d, own_kv, own_kv, {"seq": base + mate(d)})
+    for i in range(12, 15):
+        loads[i].wait()
+    entries = rk.shape[0]
+    chunk = min(hd, entries // kv)
+    at_row = lax.broadcasted_iota(jnp.int32, (chunk, chunk * kv), 0)
+    at_column = lax.broadcasted_iota(jnp.int32, (chunk, chunk * kv), 1)
+    length_here = lens_ref[request]
+    kept = []
+    for k in range(kv):
+        place_of = jnp.where(at_column == at_row * kv + k, 1.0, 0.0).astype(BF16)
+        pieces = []
+        for c in range(entries // kv // chunk):
+            index_row = ridx_ref[k : k + 1, c * chunk : (c + 1) * chunk]
+            flag = jnp.where(index_row < length_here, 1.0, 0.0)
+            flag = jnp.broadcast_to(flag, (16, chunk)).astype(BF16)
+            pieces.append(jnp.dot(flag, place_of, preferred_element_type=F32)[0:1, :])
+        kept.append(jnp.concatenate(pieces, axis=1))
     for d in range(1, G):
         source = mate(G - d)
-        arrive(6, d, upper.at[source], upper.at[source], {"seq": base + source})
-
-    entries = rk.shape[0]
-    entry = lax.broadcasted_iota(jnp.int32, (1, entries), 1)
-    kept = ridx_ref[...] < lens_ref[request]
+        there = upper.at[source, pl.ds(0, kv)]
+        arrive(6, d, there, there, {"seq": base + source})
+
     stats = []
     for k in range(kv):
-        allowed = jnp.logical_and(jnp.bitwise_and(entry, kv - 1) == k, kept)
+        allowed = kept[k] > 0.5
         queries = upper[:, k].reshape(nodes * g, hd)
         blend, high, total = attend(queries, rk[...], rv[...], allowed, scale)
         stats.append((high, total))
@@ -354,19 +406,21 @@
             upart[a, k] = blend[a * rows : (a + 1) * rows].astype(BF16)
     packed = pack_stats(stats)
     for a in range(G):
-        ustat[a] = packed[a * rows : (a + 1) * rows]
+        upart[a, kv] = packed[a * rows : (a + 1) * rows]
     for d in range(1, G):
         target = mate(d)
         send(7, d, upart.at[target], ugpart.at[place], {"seq": base + target})
-        send(8, d, ustat.at[target], ugstat.at[place], {"seq": base + target})
     ugpart[place] = upart[place]
-    ugstat[place] = ustat[place]
+    for d in range(1, G):
+        source = mate(G - d)
+        there = upper.at[source, pl.ds(kv, 1)]
+        arrive(8, d, there, there, {"seq": base + source})
     form[kv, : nodes * g, :] = upper[:, kv].reshape(nodes * g, hd).astype(F32)
+    trees = tree_part(own_queries, form.at[kv], tree_mask)
     for d in range(1, G):
         source = mate(G - d)
         arrive(7, d, upart.at[source], ugpart.at[source], {"seq": base + source})
-        arrive(8, d, ustat.at[source], ugstat.at[source], {"seq": base + source})
-    done = finish(ugstat, ugpart, G, own_queries, form.at[kv])
+    done = finish(ugpart, G, trees)
     for k in range(kv):
         form[k, :rows, :] = done[k]
         for j in range(g):
@@ -408,37 +462,50 @@
     cv = cache_values.reshape(R, part * kv, hd)
     rk = retained_keys.reshape(entries, hd)
     rv = retained_values.reshape(entries, hd)
-    ridx = retained_index.reshape(1, entries)
+    ridx = retained_index[0].T
     gain = norm_gain.reshape(1, features)
     vmem = pl.BlockSpec(memory_space=pltpu.VMEM)
     hbm = pl.BlockSpec(memory_space=pl.ANY)
-    big = (ck, cv, out_weight, w_key_up, w_value_up, w_query_up, rk, rv)
-    return pl.pallas_call(
+    big = (
+        query_low,
+        key_tree_low,
+        value_tree_low,
+        ck,
+        cv,
+        ancestors,
+        out_weight,
+        tree_hidden,
+        gain,
+        w_key_up,
+        w_value_up,
+        w_query_up,
+        ridx,
+        rk,
+        rv,
+    )
+    outs = pl.pallas_call(
         functools.partial(kernel, (S, T, R, own, kv, g, hd)),
         out_shape=(
             jax.ShapeDtypeStruct((M, features), F32),
             jax.ShapeDtypeStruct((own, row_width), F32),
         ),
-        in_specs=[pl.BlockSpec(memory_space=pltpu.SMEM)] + [vmem] * 7 + [hbm] * 8,
+        in_specs=[pl.BlockSpec(memory_space=pltpu.HBM)] + [hbm] * len(big),
         out_specs=(vmem, vmem),
-        scratch_shapes=[pltpu.VMEM(x.shape, x.dtype) for x in big]
+        scratch_shapes=[pltpu.SMEM((R,), jnp.int32)]
+        + [pltpu.VMEM(x.shape, x.dtype) for x in big]
         + [
             pltpu.VMEM((kv + 1, M * g, hd), F32),
             pltpu.VMEM((S, kv + 1, rows, hd), BF16),
-            pltpu.VMEM((S, kv, rows, hd), BF16),
-            pltpu.VMEM((S, rows, hd), F32),
-            pltpu.VMEM((S, kv, rows, hd), BF16),
-            pltpu.VMEM((S, rows, hd), F32),
+            pltpu.VMEM((S, kv + 1, rows, hd), BF16),
+            pltpu.VMEM((S, kv + 1, rows, hd), BF16),
             pltpu.VMEM((S, kv, rows, hd), BF16),
             pltpu.VMEM((T, M, features), BF16),
             pltpu.VMEM((S, kv + 1, rows, hd), BF16),
             pltpu.VMEM((S, kv + 1, rows, hd), BF16),
             pltpu.VMEM((G, kv + 1, rows, hd), BF16),
-            pltpu.VMEM((G, kv, rows, hd), BF16),
-            pltpu.VMEM((G, rows, hd), F32),
-            pltpu.VMEM((G, kv, rows, hd), BF16),
-            pltpu.VMEM((G, rows, hd), F32),
-            pltpu.SemaphoreType.DMA((len(big),)),
+            pltpu.VMEM((G, kv + 1, rows, hd), BF16),
+            pltpu.VMEM((G, kv + 1, rows, hd), BF16),
+            pltpu.SemaphoreType.DMA((1 + len(big),)),
             pltpu.SemaphoreType.DMA((9, max(S, T))),
             pltpu.SemaphoreType.DMA((9, max(S, T))),
         ],
@@ -448,15 +515,20 @@
         name="two_layers",
     )(
         cache_lengths,
-        query_low,
-        key_tree_low,
-        value_tree_low,
-        tree_hidden,
-        ancestors,
-        gain,
-        ridx,
         *big,
     )
+
+    def settle(a_ref, b_ref, c_ref, d_ref):
+        c_ref[...] = a_ref[...]
+        d_ref[...] = b_ref[...]
+
+    return pl.pallas_call(
+        settle,
+        out_shape=tuple(jax.ShapeDtypeStruct(x.shape, x.dtype) for x in outs),
+        in_specs=[vmem] * 2,
+        out_specs=(vmem, vmem),
+        name="settle",
+    )(*outs)
 
 
 def solution(mesh):

time: 49 us -> 44.3 us (0.904)
  local copies, waits for them, and re-layouts: 4.4 us -> 0 us
    unnamed x3 -> x0, local copies, waits for them, and re-layouts: 3.62 us -> none
    pallas_call x1, Pallas kernels: 43 us -> 41.3 us  [shards(): pl.pallas_call(functools.partial(kernel, (S, T, R, own, kv, g, hd)), out_...]
    pallas_call x0 -> x1, Pallas kernels: none -> 1.48 us  [shards(): pl.pallas_call(settle, out_shape=tuple((jax.ShapeDtypeStruct(x.shape, x.d...]
    reshape x1 -> x0, local copies, waits for them, and re-layouts: 0.78 us -> none  [shards(): ridx = retained_index.reshape(1, entries)]
where the time goes in v2:
time: 44.3 us; the launch traced here: 44.1 us
  Pallas kernels  42.8 us (97%)
  between operations  1.29 us (3%)
    pallas_call x1, Pallas kernels, shards(): pl.pallas_call(functools.partial(kernel, (S, T, R, own, kv, g, hd)), out_...  41.3 us
    pallas_call x1, Pallas kernels, shards(): pl.pallas_call(settle, out_shape=tuple((jax.ShapeDtypeStruct(x.shape, x.d...  1.48 us

profile of v2, /device:TPU:0, one launch (start us, length us, event | category | flops | bytes accessed | tf_op | source)
XLA Modules:
  0.0 44.1 jit_solution(9597755383497335947)
XLA Ops:
  1.3 41.3 %two_layers.1 = (f32[16,1024]{1,0:T(8,128)}, f32[2,2048]{1,0:T(2,128)}) custom-call(s32[1]{0:T(128)S(6)} %copy.18.lens_hbm, bf16[2,2048]{1,0:T(2,128)(2,1)} %q_hbm.1, bf16[2,256]{1,0:T(2,128)(2,1)} %k_hbm.1, bf16[2,256]{1,0:T(2,128)(2,1)} %v_hbm.1, bf16[1,2048,128]{2,1,0:T(8,128)(2,1)} %bitcast.8, bf16[1,2048,128]{2,1,0:T(8,128)(2,1)} %bitcast.9, ...), custom_call_target="tpu_custom_call" | custom-call | tf_op jit(solution)/shard_map/two_layers/pallas_call | solution.py:486
  42.6 1.5 %settle.1 = (f32[16,1024]{1,0:T(8,128)}, f32[2,2048]{1,0:T(2,128)}) custom-call(f32[16,1024]{1,0:T(8,128)} %get-tuple-element.4.a_ref, f32[2,2048]{1,0:T(2,128)} %get-tuple-element.5.b_ref), custom_call_target="tpu_custom_call" | custom-call | tf_op jit(solution)/shard_map/settle/pallas_call | solution.py:525
